TPU v7x, 32 devices: a whole 2x2x4 slice. The times are simulated.
32 devices in a mesh: dp: 8 (over z, y), mp: 4 (over x, core).
Axes of the slice: x: 2, y: 2, z: 4, core: 2. Of those that a mesh axis runs over, the one named last changes fastest.
Arguments:
- features: bfloat16 [3, 512, 16384], P(None, 'mp', 'dp'), may hold values from -6 to 6
- weights: bfloat16 [11, 512, 512], P(None, 'mp'), may hold values from -0.25 to 0.25
- sample_owner: int32 [3, 16384, 1], P(None, 'dp'), may hold values from 0 to 7; in each aligned block of 2048 rows (0 to 2047, 2048 to 4095, ..., all dimensions but the last counted through in order) at most 512 rows name the same one
- sample_row: int32 [3, 16384], P(None, 'dp'), may hold values from 0 to 2047
- edge_src: int32 [8, 16384], P(None, 'dp'), may hold values from 0 to 2047
- edge_dst: int32 [8, 16384], P(None, 'dp'), may hold values from 0 to 127
- edge_count: int32 [8, 8], P(None, 'dp'), may hold values from 128 to 2048
Outputs:
- updated: bfloat16 [3, 512, 1024], P(None, 'mp', 'dp')
Inputs may be any that keep to these rules, and one draw needn't show every extreme that they name: `sample_owner`: among the 2048 entries of one node type in one block no owner appears more than 512 times; some owner appears exactly 512 times in some blocks.
All inputs are finite; a program needn't handle non-finite values.
Results may differ from a plain program's by a relative error of at most 0.0064.
Values may be sent and summed in bfloat16 or wider, within the bound.
A program may use at most 64 MiB of HBM per device.

v0:
```python
import math
import jax
import jax.numpy as jnp
from jax import lax
from jax.sharding import PartitionSpec as P

RELS = 8
SEEDS = 128
RELATION_SOURCE = (0, 1, 0, 1, 2, 0, 2, 1)
MATRIX_TARGET = (1, 0, 0, 2, 1, 2, 0, 1, 0, 1, 2)


def pick_columns(table, index):
    count = index.shape[0]
    block_size = math.gcd(count, 512)
    row_ids = jnp.arange(table.shape[1], dtype=jnp.int32)[:, None]

    def one_block(block):
        chosen = (row_ids == block[None, :]).astype(jnp.bfloat16)
        return jnp.dot(table, chosen, preferred_element_type=jnp.float32).astype(jnp.bfloat16)

    picked = lax.map(one_block, index.reshape(count // block_size, block_size))
    return picked.transpose(1, 0, 2).reshape(table.shape[0], count)


def serve_kind(kind_table, requested):
    picked = pick_columns(kind_table, requested.reshape(-1))
    picked = picked.reshape(kind_table.shape[0], requested.shape[0], requested.shape[1])
    return lax.all_to_all(picked, "dp", split_axis=1, concat_axis=1, tiled=True)


def contract_first(left, right):
    return lax.dot_general(
        left, right, (((0,), (0,)), ((), ())), preferred_element_type=jnp.float32
    )


def per_device(features, weights, sample_owner, sample_row, edge_src, edge_dst, edge_count):
    groups = lax.axis_size("dp")
    node_kinds = features.shape[0]
    width_here = features.shape[1]
    sampled = sample_row.shape[1]
    capacity = 2 * sampled // groups
    owners = sample_owner[:, :, 0]
    owner_hot = (owners[:, :, None] == jnp.arange(groups, dtype=jnp.int32)[None, None, :]).astype(
        jnp.float32
    )
    block_size = math.gcd(sampled, 512)
    blocks = owner_hot.reshape(node_kinds, sampled // block_size, block_size, groups)
    block_ids = jnp.arange(block_size, dtype=jnp.int32)
    lower = (block_ids[:, None] >= block_ids[None, :]).astype(jnp.float32)
    within = jnp.einsum("ij,tbjo->tbio", lower, blocks, precision=lax.Precision.HIGHEST)
    totals = jnp.sum(blocks, axis=2)
    before = jnp.cumsum(totals, axis=1) - totals
    inclusive = (within + before[:, :, None, :]).reshape(node_kinds, sampled, groups)
    slot_rank = jnp.sum((inclusive - 1.0) * owner_hot, axis=2).astype(jnp.int32)
    position = owners * capacity + slot_rank
    rank_hot = (
        slot_rank[:, :, None] == jnp.arange(capacity, dtype=jnp.int32)[None, None, :]
    ).astype(jnp.float32)
    weighted_owner = owner_hot * sample_row[:, :, None].astype(jnp.float32)
    requests = jnp.einsum(
        "tio,tik->tok", weighted_owner, rank_hot, precision=lax.Precision.HIGHEST
    ).astype(jnp.int32)
    fetched_parts = []
    for node_kind in range(node_kinds):
        fetched_parts.append(
            serve_kind(
                features[node_kind],
                lax.all_to_all(requests[node_kind], "dp", split_axis=0, concat_axis=0, tiled=True),
            )
        )
    fetched = jnp.stack(fetched_parts)
    fetched = fetched.reshape(node_kinds, width_here, groups * capacity)
    gathered = jnp.stack(
        [pick_columns(fetched[node_kind], position[node_kind]) for node_kind in range(node_kinds)]
    )
    edge_total = edge_src.shape[1]
    seed_ids = jnp.arange(SEEDS, dtype=jnp.int32)[:, None]
    slot_ids = jnp.arange(edge_total, dtype=jnp.int32)
    messages = []
    for relation in range(RELS):
        live_edge = slot_ids < edge_count[relation, 0]
        target = jnp.where(live_edge, edge_dst[relation], -1)
        dst_hot = (seed_ids == target[None, :]).astype(jnp.bfloat16)
        sources = pick_columns(gathered[RELATION_SOURCE[relation]], edge_src[relation])
        summed = lax.dot_general(
            sources, dst_hot, (((1,), (1,)), ((), ())), preferred_element_type=jnp.float32
        )
        degree = jnp.sum(dst_hot, axis=1, dtype=jnp.float32)
        messages.append((summed / jnp.maximum(degree, 1.0)[None, :]).astype(jnp.bfloat16))
    for node_kind in range(node_kinds):
        messages.append(gathered[node_kind, :, :SEEDS])
    stacked = jnp.stack(messages)
    full_width = weights.shape[2]
    partial_sums = [jnp.zeros((full_width, SEEDS), jnp.float32) for node_kind in range(node_kinds)]
    for matrix in range(stacked.shape[0]):
        partial_sums[MATRIX_TARGET[matrix]] = partial_sums[MATRIX_TARGET[matrix]] + contract_first(
            weights[matrix], stacked[matrix]
        )
    typed = lax.psum_scatter(jnp.stack(partial_sums), "mp", scatter_dimension=1, tiled=True)
    return jax.nn.relu(typed).astype(jnp.bfloat16)


def solution(mesh):
    return jax.shard_map(
        per_device,
        mesh=mesh,
        in_specs=(
            P(None, "mp", "dp"),
            P(None, "mp", None),
            P(None, "dp", None),
            P(None, "dp"),
            P(None, "dp"),
            P(None, "dp"),
            P(None, "dp"),
        ),
        out_specs=P(None, "mp", "dp"),
        check_vma=False,
    )
```

profile of v0, /device:TPU:0, one launch (start us, length us, event | category | flops | bytes accessed | tf_op | source)
XLA Modules:
  0.0 245.6 jit_solution(14992279231206325996)
XLA Ops:
  9.4 4.3 %fusion.227 = s32[3,8,512]{2,1,0:T(8,128)S(1)} fusion(s32[3,2048]{1,0:T(4,128)S(1)} %bitcast.375, f32[3,2048]{1,0:T(4,128)S(1)} %convert_element_type.199, s32[3,2048]{1,0:T(4,128)S(1)} %bitcast.394), kind=kOutput, calls=%fused_computation.161 | convolution fusion | flops 305246208 | bytes 122880 | tf_op jit(solution)/shard_map/tio,tik->tok/dot_general | solution.py:62
  14.4 7.3 %all-to-all-start = ((s32[8,1,512]{2,1,0:T(1,128)}), s32[8,1,512]{2,1,0:T(1,128)S(1)}, u32[]{:S(2)}, u32[]{:S(2)}) async-start(s32[8,1,512]{2,1,0:T(1,128)} %copy.32), calls=%async_computation | async-start | bytes 32768 | tf_op jit(solution)/shard_map/all_to_all | solution.py:70
  22.5 5.1 %compare_select_fusion.5 = (s32[1,2048]{1,0:T(1,128)S(1)}, s32[1,2048]{1,0:T(1,128)S(1)}, s32[1,2048]{1,0:T(1,128)S(1)}, s32[1,2048]{1,0:T(1,128)S(1)}, s32[1,20...) fusion(s32[8,2048]{1,0:T(8,128)S(1)} %copy-done.14, s32[]{:T(128)} %bitcast.33, ...), kind=kLoop, calls=%fused_computation.252 | loop fusion | flops 32768 | bytes 131104 | tf_op jit(solution)/shard_map/jit(_where)/select_n | solution.py:84
  29.9 6.0 %all-to-all-start.2 = ((s32[8,1,512]{2,1,0:T(1,128)}), s32[8,1,512]{2,1,0:T(1,128)S(1)}, u32[]{:S(2)}, u32[]{:S(2)}) async-start(s32[8,1,512]{2,1,0:T(1,128)} %copy.35), calls=%async_computation.2 | async-start | bytes 32768 | tf_op jit(solution)/shard_map/all_to_all | solution.py:70
  36.9 5.6 %all-to-all-done.2 = s32[8,1,512]{2,1,0:T(1,128)S(1)} async-done(((s32[8,1,512]{2,1,0:T(1,128)}), s32[8,1,512]{2,1,0:T(1,128)S(1)}, u32[]{:S(2)}, u32[]{:S(2)}) %all-to-all-start.2) | async-done | bytes 16416 | tf_op jit(solution)/shard_map/all_to_all | solution.py:70
  47.0 11.4 %while.154 = (s32[]{:T(128)}, bf16[8,128,512]{1,2,0:T(8,128)(2,1)}, s32[8,512]{1,0:T(8,128)S(1)}, bf16[128,2048]{1,0:T(8,128)(2,1)S(1)}, s32[]{:T(128)}) while((s32[]{:T(128)}, bf16[8,128,512]{1,2,0:T(8,128)(2,1)}, s32[8,512]{1,0:T(8,128)S(1)}, bf16[128,2048]{1,0:T(8,128)(2,1)S(1)}, s32[]{:T(128)}) %tuple.315), condition=%wide.region_4.5_spmd.clone, body=%wide.region_3.4_spmd.clone.sunk | while | flops 270598144 | bytes 662081 | solution.py:22
  58.3 5.9 %all-to-all-start.1 = ((bf16[128,8,512]{0,2,1:T(8,128)(2,1)}), bf16[128,8,512]{0,2,1:T(8,128)(2,1)S(1)}, u32[]{:S(2)}, u32[]{:S(2)}) async-start(bf16[128,8,512]{0,2,1:T(8,128)(2,1)} %bitcast.5), calls=%async_computation.1 | async-start | bytes 2097152 | tf_op jit(solution)/shard_map/all_to_all | solution.py:29
  65.4 11.3 %while.157 = (s32[]{:T(128)}, bf16[8,128,512]{1,2,0:T(8,128)(2,1)}, s32[8,512]{1,0:T(8,128)S(1)}, bf16[128,2048]{1,0:T(8,128)(2,1)S(1)}, s32[]{:T(128)}) while((s32[]{:T(128)}, bf16[8,128,512]{1,2,0:T(8,128)(2,1)}, s32[8,512]{1,0:T(8,128)S(1)}, bf16[128,2048]{1,0:T(8,128)(2,1)S(1)}, s32[]{:T(128)}) %tuple.314), condition=%wide.region_11.12_spmd.clone, body=%wide.region_10.11_spmd.clone.sunk | while | flops 270598144 | bytes 662081 | solution.py:22
  76.8 11.2 %all-to-all-done.1 = bf16[128,8,512]{0,2,1:T(8,128)(2,1)S(1)} async-done(((bf16[128,8,512]{0,2,1:T(8,128)(2,1)}), bf16[128,8,512]{0,2,1:T(8,128)(2,1)S(1)}, u32[]{:S(2)}, u32[]{:S(2)}) %all-to-all-start.1) | async-done | bytes 1048608 | tf_op jit(solution)/shard_map/all_to_all | solution.py:29
  88.0 3.6 %all-to-all-start.3 = ((bf16[128,8,512]{0,2,1:T(8,128)(2,1)}), bf16[128,8,512]{0,2,1:T(8,128)(2,1)S(1)}, u32[]{:S(2)}, u32[]{:S(2)}) async-start(bf16[128,8,512]{0,2,1:T(8,128)(2,1)} %bitcast.16), calls=%async_computation.3 | async-start | bytes 2097152 | tf_op jit(solution)/shard_map/all_to_all | solution.py:29
  92.7 11.3 %while.160 = (s32[]{:T(128)}, bf16[8,128,512]{1,2,0:T(8,128)(2,1)}, s32[8,512]{1,0:T(8,128)S(1)}, bf16[128,2048]{1,0:T(8,128)(2,1)S(1)}, s32[]{:T(128)}) while((s32[]{:T(128)}, bf16[8,128,512]{1,2,0:T(8,128)(2,1)}, s32[8,512]{1,0:T(8,128)S(1)}, bf16[128,2048]{1,0:T(8,128)(2,1)S(1)}, s32[]{:T(128)}) %tuple.313), condition=%wide.region_18.19_spmd.clone, body=%wide.region_17.18_spmd.clone.sunk | while | flops 270598144 | bytes 662081 | solution.py:22
  105.4 10.5 %while.155 = (s32[]{:T(128)}, bf16[4,128,512]{1,2,0:T(8,128)(2,1)S(1)}, s32[4,512]{1,0:T(4,128)S(1)}, bf16[128,4096]{1,0:T(8,128)(2,1)}, s32[]{:T(128)}) while((s32[]{:T(128)}, bf16[4,128,512]{1,2,0:T(8,128)(2,1)S(1)}, s32[4,512]{1,0:T(4,128)S(1)}, bf16[128,4096]{1,0:T(8,128)(2,1)}, s32[]{:T(128)}) %tuple.267), condition=%wide.region_6.7_spmd.clone, body=%wide.region_5.6_spmd.clone.sunk | while | flops 541130752 | bytes 1185861 | solution.py:22
  116.9 5.9 %all-to-all-start.5 = ((bf16[128,8,512]{0,2,1:T(8,128)(2,1)}), bf16[128,8,512]{0,2,1:T(8,128)(2,1)S(1)}, u32[]{:S(2)}, u32[]{:S(2)}) async-start(bf16[128,8,512]{0,2,1:T(8,128)(2,1)} %bitcast.27), calls=%async_computation.5 | async-start | bytes 2097152 | tf_op jit(solution)/shard_map/all_to_all | solution.py:29
  124.4 10.5 %while.158 = (s32[]{:T(128)}, bf16[4,128,512]{1,2,0:T(8,128)(2,1)S(1)}, s32[4,512]{1,0:T(4,128)S(1)}, bf16[128,4096]{1,0:T(8,128)(2,1)}, s32[]{:T(128)}) while((s32[]{:T(128)}, bf16[4,128,512]{1,2,0:T(8,128)(2,1)S(1)}, s32[4,512]{1,0:T(4,128)S(1)}, bf16[128,4096]{1,0:T(8,128)(2,1)}, s32[]{:T(128)}) %tuple.276), condition=%wide.region_13.14_spmd.clone, body=%wide.region_12.13_spmd.clone.sunk | while | flops 541130752 | bytes 1185861 | solution.py:22
  135.0 3.4 %while.156 = (s32[]{:T(128)}, bf16[4,128,512]{1,2,0:T(8,128)(2,1)S(1)}, s32[4,512]{1,0:T(4,128)S(1)}, bf16[128,2048]{1,0:T(8,128)(2,1)S(1)}, s32[]{:T(128)}) while((s32[]{:T(128)}, bf16[4,128,512]{1,2,0:T(8,128)(2,1)S(1)}, s32[4,512]{1,0:T(4,128)S(1)}, bf16[128,2048]{1,0:T(8,128)(2,1)S(1)}, s32[]{:T(128)}) %tuple.308), condition=%wide.region_8.9_spmd.clone, body=%wide.region_7.8_spmd.clone.sunk | while | flops 270598144 | bytes 661573 | solution.py:22
  139.5 7.6 %while.159 = (s32[]{:T(128)}, bf16[4,128,512]{1,2,0:T(8,128)(2,1)S(1)}, s32[4,512]{1,0:T(4,128)S(1)}, bf16[128,2048]{1,0:T(8,128)(2,1)}, s32[]{:T(128)}) while((s32[]{:T(128)}, bf16[4,128,512]{1,2,0:T(8,128)(2,1)S(1)}, s32[4,512]{1,0:T(4,128)S(1)}, bf16[128,2048]{1,0:T(8,128)(2,1)}, s32[]{:T(128)}) %tuple.300), condition=%wide.region_15.16_spmd.clone, body=%wide.region_14.15_spmd.clone.sunk | while | flops 270598144 | bytes 661573 | solution.py:22
  148.5 5.6 %while.161 = (s32[]{:T(128)}, bf16[4,128,512]{1,2,0:T(8,128)(2,1)S(1)}, s32[4,512]{1,0:T(4,128)S(1)}, bf16[128,4096]{1,0:T(8,128)(2,1)S(1)}, s32[]{:T(128)}) while((s32[]{:T(128)}, bf16[4,128,512]{1,2,0:T(8,128)(2,1)S(1)}, s32[4,512]{1,0:T(4,128)S(1)}, bf16[128,4096]{1,0:T(8,128)(2,1)S(1)}, s32[]{:T(128)}) %tuple.285), condition=%wide.region_20.21_spmd.clone, body=%wide.region_19.20_spmd.clone.sunk | while | flops 541130752 | bytes 1185861 | solution.py:22
  155.2 7.6 %while.162 = (s32[]{:T(128)}, bf16[4,128,512]{1,2,0:T(8,128)(2,1)S(1)}, s32[4,512]{1,0:T(4,128)S(1)}, bf16[128,2048]{1,0:T(8,128)(2,1)}, s32[]{:T(128)}) while((s32[]{:T(128)}, bf16[4,128,512]{1,2,0:T(8,128)(2,1)S(1)}, s32[4,512]{1,0:T(4,128)S(1)}, bf16[128,2048]{1,0:T(8,128)(2,1)}, s32[]{:T(128)}) %tuple.303), condition=%wide.region_22.23_spmd.clone, body=%wide.region_21.22_spmd.clone.sunk | while | flops 270598144 | bytes 661573 | solution.py:22
  163.7 3.4 %while.163 = (s32[]{:T(128)}, bf16[4,128,512]{1,2,0:T(8,128)(2,1)S(1)}, s32[4,512]{1,0:T(4,128)S(1)}, bf16[128,2048]{1,0:T(8,128)(2,1)S(1)}, s32[]{:T(128)}) while((s32[]{:T(128)}, bf16[4,128,512]{1,2,0:T(8,128)(2,1)S(1)}, s32[4,512]{1,0:T(4,128)S(1)}, bf16[128,2048]{1,0:T(8,128)(2,1)S(1)}, s32[]{:T(128)}) %tuple.311), condition=%wide.region_25.26_spmd.clone, body=%wide.region_24.25_spmd.clone.sunk | while | flops 270598144 | bytes 661573 | solution.py:22
  167.8 7.5 %while.164 = (s32[]{:T(128)}, bf16[4,128,512]{1,2,0:T(8,128)(2,1)S(1)}, s32[4,512]{1,0:T(4,128)S(1)}, bf16[128,2048]{1,0:T(8,128)(2,1)}, s32[]{:T(128)}) while((s32[]{:T(128)}, bf16[4,128,512]{1,2,0:T(8,128)(2,1)S(1)}, s32[4,512]{1,0:T(4,128)S(1)}, bf16[128,2048]{1,0:T(8,128)(2,1)}, s32[]{:T(128)}) %tuple.291), condition=%wide.region_28.29_spmd.clone, body=%wide.region_27.28_spmd.clone.sunk | while | flops 270598144 | bytes 661573 | solution.py:22
  176.2 3.4 %while.165 = (s32[]{:T(128)}, bf16[4,128,512]{1,2,0:T(8,128)(2,1)S(1)}, s32[4,512]{1,0:T(4,128)S(1)}, bf16[128,2048]{1,0:T(8,128)(2,1)S(1)}, s32[]{:T(128)}) while((s32[]{:T(128)}, bf16[4,128,512]{1,2,0:T(8,128)(2,1)S(1)}, s32[4,512]{1,0:T(4,128)S(1)}, bf16[128,2048]{1,0:T(8,128)(2,1)S(1)}, s32[]{:T(128)}) %tuple.309), condition=%wide.region_31.32_spmd.clone, body=%wide.region_30.31_spmd.clone.sunk | while | flops 270598144 | bytes 661573 | solution.py:22
  180.5 5.7 %while.166 = (s32[]{:T(128)}, bf16[4,128,512]{1,2,0:T(8,128)(2,1)}, s32[4,512]{1,0:T(4,128)S(1)}, bf16[128,2048]{1,0:T(8,128)(2,1)S(1)}, s32[]{:T(128)}) while((s32[]{:T(128)}, bf16[4,128,512]{1,2,0:T(8,128)(2,1)}, s32[4,512]{1,0:T(4,128)S(1)}, bf16[128,2048]{1,0:T(8,128)(2,1)S(1)}, s32[]{:T(128)}) %tuple.310), condition=%wide.region_34.35_spmd.clone, body=%wide.region_33.34_spmd.clone.sunk | while | flops 270598144 | bytes 662081 | solution.py:22
  186.3 7.9 %while.167 = (s32[]{:T(128)}, bf16[4,128,512]{1,2,0:T(8,128)(2,1)S(1)}, s32[4,512]{1,0:T(4,128)S(1)}, bf16[128,2048]{1,0:T(8,128)(2,1)}, s32[]{:T(128)}) while((s32[]{:T(128)}, bf16[4,128,512]{1,2,0:T(8,128)(2,1)S(1)}, s32[4,512]{1,0:T(4,128)S(1)}, bf16[128,2048]{1,0:T(8,128)(2,1)}, s32[]{:T(128)}) %tuple.312), condition=%wide.region_37.38_spmd.clone, body=%wide.region_36.37_spmd.clone.sunk | while | flops 270598144 | bytes 661573 | solution.py:22
  212.6 24.5 %reduce-scatter.2.cloned.1.call-done = f32[3,128,128]{1,2,0:T(8,128)} async-done(((f32[3,512,128]{1,2,0:T(8,128)}), f32[3,128,128]{1,2,0:T(8,128)}) %reduce-scatter.2.cloned.1.call-update) | async-done | bytes 196624 | tf_op jit(solution)/shard_map/reduce_scatter | solution.py:101
  (259 shorter events, 151.0 us)
Async XLA Ops:
  9.4 12.3 %copy-start.13 = (s32[3,2048,1]{1,2,0:T(1,128)S(1)}, s32[3,2048,1]{1,2,0:T(1,128)}, u32[]{:S(2)}) copy-start(s32[3,2048,1]{1,2,0:T(1,128)} %param.37) | copy-start | bytes 73732
  9.4 12.4 %copy-start.16 = (s32[8,1]{0,1:T(1,128)S(1)}, s32[8,1]{0,1:T(1,128)}, u32[]{:S(2)}) copy-start(s32[8,1]{0,1:T(1,128)} %param.41) | copy-start | bytes 100
  9.4 13.1 %copy-start.14 = (s32[8,2048]{1,0:T(8,128)S(1)}, s32[8,2048]{1,0:T(8,128)}, u32[]{:S(2)}) copy-start(s32[8,2048]{1,0:T(8,128)} %param.40) | copy-start | bytes 196612
  9.4 18.3 %copy-start = (bf16[3,128,2048]{2,1,0:T(8,128)(2,1)S(1)}, bf16[3,128,2048]{2,1,0:T(8,128)(2,1)}, u32[]{:S(2)}) copy-start(bf16[3,128,2048]{2,1,0:T(8,128)(2,1)} %param.35) | copy-start | bytes 4718596
  14.4 15.5 %all-to-all-start = ((s32[8,1,512]{2,1,0:T(1,128)}), s32[8,1,512]{2,1,0:T(1,128)S(1)}, u32[]{:S(2)}, u32[]{:S(2)}) async-start(s32[8,1,512]{2,1,0:T(1,128)} %copy.32), calls=%async_computation | async-start | bytes 32768 | tf_op jit(solution)/shard_map/all_to_all | solution.py:70
  27.7 8.2 %copy-start.15 = (s32[8,2048]{1,0:T(8,128)S(1)}, s32[8,2048]{1,0:T(8,128)}, u32[]{:S(2)}) copy-start(s32[8,2048]{1,0:T(8,128)} %param.39) | copy-start | bytes 196612
  29.9 12.6 %all-to-all-start.2 = ((s32[8,1,512]{2,1,0:T(1,128)}), s32[8,1,512]{2,1,0:T(1,128)S(1)}, u32[]{:S(2)}, u32[]{:S(2)}) async-start(s32[8,1,512]{2,1,0:T(1,128)} %copy.35), calls=%async_computation.2 | async-start | bytes 32768 | tf_op jit(solution)/shard_map/all_to_all | solution.py:70
  42.5 15.8 %all-to-all-start.4 = ((s32[8,1,512]{2,1,0:T(1,128)}), s32[8,1,512]{2,1,0:T(1,128)S(1)}, u32[]{:S(2)}, u32[]{:S(2)}) async-start(s32[8,1,512]{2,1,0:T(1,128)} %copy.38), calls=%async_computation.4 | async-start | bytes 32768 | tf_op jit(solution)/shard_map/all_to_all | solution.py:70
  58.3 29.7 %all-to-all-start.1 = ((bf16[128,8,512]{0,2,1:T(8,128)(2,1)}), bf16[128,8,512]{0,2,1:T(8,128)(2,1)S(1)}, u32[]{:S(2)}, u32[]{:S(2)}) async-start(bf16[128,8,512]{0,2,1:T(8,128)(2,1)} %bitcast.5), calls=%async_computation.1 | async-start | bytes 2097152 | tf_op jit(solution)/shard_map/all_to_all | solution.py:29
  88.0 28.9 %all-to-all-start.3 = ((bf16[128,8,512]{0,2,1:T(8,128)(2,1)}), bf16[128,8,512]{0,2,1:T(8,128)(2,1)S(1)}, u32[]{:S(2)}, u32[]{:S(2)}) async-start(bf16[128,8,512]{0,2,1:T(8,128)(2,1)} %bitcast.16), calls=%async_computation.3 | async-start | bytes 2097152 | tf_op jit(solution)/shard_map/all_to_all | solution.py:29
  116.9 30.7 %all-to-all-start.5 = ((bf16[128,8,512]{0,2,1:T(8,128)(2,1)}), bf16[128,8,512]{0,2,1:T(8,128)(2,1)S(1)}, u32[]{:S(2)}, u32[]{:S(2)}) async-start(bf16[128,8,512]{0,2,1:T(8,128)(2,1)} %bitcast.27), calls=%async_computation.5 | async-start | bytes 2097152 | tf_op jit(solution)/shard_map/all_to_all | solution.py:29
  122.8 114.3 %reduce-scatter.2.cloned.1.call-start = ((), (), s32[]{:S(2)}) async-start(), calls=%async_computation.7 | async-start | bytes 983040 | tf_op jit(solution)/shard_map/reduce_scatter | solution.py:101
  124.4 10.6 %copy-start.10 = (bf16[128,2048]{1,0:T(8,128)(2,1)S(1)}, bf16[128,2048]{1,0:T(8,128)(2,1)}, u32[]{:S(2)}) copy-start(bf16[128,2048]{1,0:T(8,128)(2,1)} %copy.44) | copy-start | bytes 1572868
  138.4 1.1 copy-start.1
  147.1 0.8 copy-start.3
  155.2 7.7 %copy-start.12 = (bf16[128,2048]{1,0:T(8,128)(2,1)S(1)}, bf16[128,2048]{1,0:T(8,128)(2,1)}, u32[]{:S(2)}) copy-start(bf16[128,2048]{1,0:T(8,128)(2,1)} %get-tuple-element.1258) | copy-start | bytes 1572868
  162.8 0.8 copy-start.5
  167.0 0.8 copy-start.6
  167.1 8.4 %copy-start.11 = (bf16[128,2048]{1,0:T(8,128)(2,1)S(1)}, bf16[128,2048]{1,0:T(8,128)(2,1)}, u32[]{:S(2)}) copy-start(bf16[128,2048]{1,0:T(8,128)(2,1)} %copy.44) | copy-start | bytes 1572868
  175.4 0.8 copy-start.8
  179.6 1.0 copy-start.9
  186.3 7.9 %copy-start.2 = (bf16[4,128,512]{1,2,0:T(8,128)(2,1)S(1)}, bf16[4,128,512]{1,2,0:T(8,128)(2,1)}, u32[]{:S(2)}) copy-start(bf16[4,128,512]{1,2,0:T(8,128)(2,1)} %copy-done.1) | copy-start | bytes 1572868
  186.3 10.1 %copy-start.4 = (bf16[4,128,512]{1,2,0:T(8,128)(2,1)S(1)}, bf16[4,128,512]{1,2,0:T(8,128)(2,1)}, u32[]{:S(2)}) copy-start(bf16[4,128,512]{1,2,0:T(8,128)(2,1)} %copy-done.3) | copy-start | bytes 1572868
  196.4 5.2 %copy-start.7 = (bf16[4,128,512]{1,2,0:T(8,128)(2,1)S(1)}, bf16[4,128,512]{1,2,0:T(8,128)(2,1)}, u32[]{:S(2)}) copy-start(bf16[4,128,512]{1,2,0:T(8,128)(2,1)} %copy-done.6) | copy-start | bytes 1572868
Sparse Core Ops, SparseCore 0:
  212.7 24.3 reduce-scatter.1
where the time goes:
time: 248 us; the launch traced here: 246 us
  matrix products  127 us (51%)
  waiting for transfers between devices  41.8 us (17%)
  starting transfers between devices  32.3 us (13%)
  local copies, waits for them, and re-layouts  18.9 us (8%)
  between operations  14 us (6%)
  other arithmetic  10.3 us (4%)
    dot_general x68, matrix products, one_block(): jnp.dot(table, chosen, preferred_element_type=jnp.float32)  105 us
    reduce_scatter x1, waiting for transfers between devices, per_device(): lax.psum_scatter(jnp.stack(partial_sums), 'mp', scatter_dimension=1, tile...  24.5 us
    dot_general x11, matrix products, contract_first(): lax.dot_general(left, right, (((0,), (0,)), ((), ())), preferred_element_...  17.3 us
    all_to_all x3, starting transfers between devices, per_device(): lax.all_to_all(requests[node_kind], 'dp', split_axis=0, concat_axis=0, ti...  16.6 us
    all_to_all x3, starting transfers between devices, serve_kind(): return lax.all_to_all(picked, 'dp', split_axis=1, concat_axis=1, tiled=True)  15.4 us
    all_to_all x3, waiting for transfers between devices, serve_kind(): return lax.all_to_all(picked, 'dp', split_axis=1, concat_axis=1, tiled=True)  11.7 us
    all_to_all x3, waiting for transfers between devices, per_device(): lax.all_to_all(requests[node_kind], 'dp', split_axis=0, concat_axis=0, ti...  5.58 us
    another operation x14, local copies, waits for them, and re-layouts  5.08 us
  transfers between devices with their start and end apart: 7, of which 4 were waited for; matrix products, arithmetic and copies ran while one was open for 34% of the time, Pallas kernels for 0%

commit v1 on v0

--- a/solution.py
+++ b/solution.py
@@ -26,7 +26,10 @@
 def serve_kind(kind_table, requested):
     picked = pick_columns(kind_table, requested.reshape(-1))
     picked = picked.reshape(kind_table.shape[0], requested.shape[0], requested.shape[1])
-    return lax.all_to_all(picked, "dp", split_axis=1, concat_axis=1, tiled=True)
+    return jnp.concatenate(
+        lax.all_to_all(jnp.stack(jnp.split(picked, lax.axis_size("dp"), axis=1)), "dp", 0, 0),
+        axis=1,
+    )
 
 
 def contract_first(left, right):

time: 248 us -> 256 us (1.032)
  matrix products: 127 us -> 112 us
  local copies, waits for them, and re-layouts: 18.9 us -> 33.1 us
  waiting for transfers between devices: 41.8 us -> 46.3 us
  other arithmetic: 10.3 us -> 13.1 us
    unnamed x39 -> x74, local copies, waits for them, and re-layouts: 3.34 us -> 19.2 us
    dot_general x68, matrix products: 105 us -> 91.2 us  [one_block(): jnp.dot(table, chosen, preferred_element_type=jnp.float32)]
    all_to_all x3, waiting for transfers between devices: 11.7 us -> 23.1 us  [serve_kind(): lax.all_to_all(jnp.stack(jnp.split(picked, lax.axis_size('dp'), axis=1)),...]
    all_to_all x3, waiting for transfers between devices: 5.58 us -> 0.01 us  [per_device(): lax.all_to_all(requests[node_kind], 'dp', split_axis=0, concat_axis=0, ti...]
    all_to_all x3, starting transfers between devices: 16.6 us -> 19.3 us  [per_device(): lax.all_to_all(requests[node_kind], 'dp', split_axis=0, concat_axis=0, ti...]
    max x8, other arithmetic: 0.05 us -> 2.71 us  [per_device(): jnp.maximum(degree, 1.0)[None, :]]
where the time goes in v1:
time: 256 us; the launch traced here: 253 us
  matrix products  112 us (44%)
  waiting for transfers between devices  46.3 us (18%)
  local copies, waits for them, and re-layouts  33.1 us (13%)
  starting transfers between devices  32.6 us (13%)
  between operations  14.1 us (6%)
  other arithmetic  13.1 us (5%)
    dot_general x68, matrix products, one_block(): jnp.dot(table, chosen, preferred_element_type=jnp.float32)  91.2 us
    reduce_scatter x1, waiting for transfers between devices, per_device(): lax.psum_scatter(jnp.stack(partial_sums), 'mp', scatter_dimension=1, tile...  23.2 us
    all_to_all x3, waiting for transfers between devices, serve_kind(): lax.all_to_all(jnp.stack(jnp.split(picked, lax.axis_size('dp'), axis=1)),...  23.1 us
    all_to_all x3, starting transfers between devices, per_device(): lax.all_to_all(requests[node_kind], 'dp', split_axis=0, concat_axis=0, ti...  19.3 us
    unnamed x74, local copies, waits for them, and re-layouts  19.2 us
    dot_general x11, matrix products, contract_first(): lax.dot_general(left, right, (((0,), (0,)), ((), ())), preferred_element_...  16.4 us
    all_to_all x3, starting transfers between devices, serve_kind(): lax.all_to_all(jnp.stack(jnp.split(picked, lax.axis_size('dp'), axis=1)),...  13.1 us
    select_n x1, other arithmetic, per_device(): target = jnp.where(live_edge, edge_dst[relation], -1)  5.25 us
  transfers between devices with their start and end apart: 7, of which 4 were waited for; matrix products, arithmetic and copies ran while one was open for 34% of the time, Pallas kernels for 0%

profile of v1, /device:TPU:0, one launch (start us, length us, event | category | flops | bytes accessed | tf_op | source)
XLA Modules:
  0.0 253.5 jit_solution(3630062770660299271)
XLA Ops:
  9.4 4.3 %fusion.227 = s32[3,8,512]{2,1,0:T(8,128)S(1)} fusion(s32[3,2048]{1,0:T(4,128)S(1)} %bitcast.502, f32[3,2048]{1,0:T(4,128)S(1)} %convert_element_type.199, s32[3,2048]{1,0:T(4,128)S(1)} %bitcast.521), kind=kOutput, calls=%fused_computation.161 | convolution fusion | flops 305246208 | bytes 122880 | tf_op jit(solution)/shard_map/tio,tik->tok/dot_general | solution.py:65
  14.4 7.3 %all-to-all-start = ((s32[8,1,512]{2,1,0:T(1,128)}), s32[8,1,512]{2,1,0:T(1,128)S(1)}, u32[]{:S(2)}, u32[]{:S(2)}) async-start(s32[8,1,512]{2,1,0:T(1,128)} %copy.32), calls=%async_computation | async-start | bytes 32768 | tf_op jit(solution)/shard_map/all_to_all | solution.py:73
  23.4 5.3 %compare_select_fusion.5 = (s32[1,2048]{1,0:T(1,128)S(1)}, s32[1,2048]{1,0:T(1,128)S(1)}, s32[1,2048]{1,0:T(1,128)S(1)}, s32[1,2048]{1,0:T(1,128)S(1)}, s32[1,20...) fusion(s32[8,2048]{1,0:T(8,128)S(1)} %copy-done.16, s32[]{:T(128)} %bitcast.60, ...), kind=kLoop, calls=%fused_computation.300 | loop fusion | flops 32768 | bytes 131104 | tf_op jit(solution)/shard_map/jit(_where)/select_n | solution.py:87
  34.5 6.0 %all-to-all-start.2 = ((s32[8,1,512]{2,1,0:T(1,128)}), s32[8,1,512]{2,1,0:T(1,128)S(1)}, u32[]{:S(2)}, u32[]{:S(2)}) async-start(s32[8,1,512]{2,1,0:T(1,128)} %copy.35), calls=%async_computation.2 | async-start | bytes 32768 | tf_op jit(solution)/shard_map/all_to_all | solution.py:73
  40.7 6.8 %while.154 = (s32[]{:T(128)}, bf16[8,128,512]{1,2,0:T(8,128)(2,1)S(1)}, s32[8,512]{1,0:T(8,128)S(1)}, bf16[128,2048]{1,0:T(8,128)(2,1)S(1)}, s32[]{:T(128)}) while((s32[]{:T(128)}, bf16[8,128,512]{1,2,0:T(8,128)(2,1)S(1)}, s32[8,512]{1,0:T(8,128)S(1)}, bf16[128,2048]{1,0:T(8,128)(2,1)S(1)}, s32[]{:T(128)}) %tuple.313), condition=%wide.region_4.5_spmd.clone, body=%wide.region_3.4_spmd.clone.sunk | while | flops 270598144 | bytes 661573 | solution.py:22
  52.7 6.0 %all-to-all-start.4 = ((s32[8,1,512]{2,1,0:T(1,128)}), s32[8,1,512]{2,1,0:T(1,128)S(1)}, u32[]{:S(2)}, u32[]{:S(2)}) async-start(s32[8,1,512]{2,1,0:T(1,128)} %copy.38), calls=%async_computation.4 | async-start | bytes 32768 | tf_op jit(solution)/shard_map/all_to_all | solution.py:73
  58.9 6.8 %while.157 = (s32[]{:T(128)}, bf16[8,128,512]{1,2,0:T(8,128)(2,1)S(1)}, s32[8,512]{1,0:T(8,128)S(1)}, bf16[128,2048]{1,0:T(8,128)(2,1)S(1)}, s32[]{:T(128)}) while((s32[]{:T(128)}, bf16[8,128,512]{1,2,0:T(8,128)(2,1)S(1)}, s32[8,512]{1,0:T(8,128)S(1)}, bf16[128,2048]{1,0:T(8,128)(2,1)S(1)}, s32[]{:T(128)}) %tuple.314), condition=%wide.region_11.12_spmd.clone, body=%wide.region_10.11_spmd.clone.sunk | while | flops 270598144 | bytes 661573 | solution.py:22
  69.6 6.0 %all-to-all-start.1 = ((bf16[8,128,1,512]{1,3,2,0:T(8,128)(2,1)}), bf16[8,128,1,512]{1,3,2,0:T(8,128)(2,1)S(1)}, u32[]{:S(2)}, u32[]{:S(2)}) async-start(bf16[8,128,1,512]{1,3,2,0:T(8,128)(2,1)} %fusion.274), calls=%async_computation.1 | async-start | bytes 2097152 | tf_op jit(solution)/shard_map/all_to_all | solution.py:30
  75.7 15.1 %while.160 = (s32[]{:T(128)}, bf16[8,128,512]{1,2,0:T(8,128)(2,1)S(1)}, s32[8,512]{1,0:T(8,128)S(1)}, bf16[128,2048]{1,0:T(8,128)(2,1)}, s32[]{:T(128)}) while((s32[]{:T(128)}, bf16[8,128,512]{1,2,0:T(8,128)(2,1)S(1)}, s32[8,512]{1,0:T(8,128)S(1)}, bf16[128,2048]{1,0:T(8,128)(2,1)}, s32[]{:T(128)}) %tuple.312), condition=%wide.region_18.19_spmd.clone, body=%wide.region_17.18_spmd.clone.sunk | while | flops 270598144 | bytes 661573 | solution.py:22
  96.2 3.7 %all-to-all-done.1 = bf16[8,128,1,512]{1,3,2,0:T(8,128)(2,1)S(1)} async-done(((bf16[8,128,1,512]{1,3,2,0:T(8,128)(2,1)}), bf16[8,128,1,512]{1,3,2,0:T(8,128)(2,1)S(1)}, u32[]{:S(2)}, u32[]{:S(2)}) %all-to-all-start.1) | async-done | bytes 1048608 | tf_op jit(solution)/shard_map/all_to_all | solution.py:30
  99.9 3.6 %all-to-all-start.3 = ((bf16[8,128,1,512]{1,3,2,0:T(8,128)(2,1)}), bf16[8,128,1,512]{1,3,2,0:T(8,128)(2,1)S(1)}, u32[]{:S(2)}, u32[]{:S(2)}) async-start(bf16[8,128,1,512]{1,3,2,0:T(8,128)(2,1)} %fusion.266), calls=%async_computation.3 | async-start | bytes 2097152 | tf_op jit(solution)/shard_map/all_to_all | solution.py:30
  105.4 5.6 %while.155 = (s32[]{:T(128)}, bf16[4,128,512]{1,2,0:T(8,128)(2,1)S(1)}, s32[4,512]{1,0:T(4,128)S(1)}, bf16[128,4096]{1,0:T(8,128)(2,1)S(1)}, s32[]{:T(128)}) while((s32[]{:T(128)}, bf16[4,128,512]{1,2,0:T(8,128)(2,1)S(1)}, s32[4,512]{1,0:T(4,128)S(1)}, bf16[128,4096]{1,0:T(8,128)(2,1)S(1)}, s32[]{:T(128)}) %tuple.267), condition=%wide.region_6.7_spmd.clone, body=%wide.region_5.6_spmd.clone.sunk | while | flops 541130752 | bytes 1185861 | solution.py:22
  112.0 17.2 %all-to-all-done.3 = bf16[8,128,1,512]{1,3,2,0:T(8,128)(2,1)S(1)} async-done(((bf16[8,128,1,512]{1,3,2,0:T(8,128)(2,1)}), bf16[8,128,1,512]{1,3,2,0:T(8,128)(2,1)S(1)}, u32[]{:S(2)}, u32[]{:S(2)}) %all-to-all-start.3) | async-done | bytes 1048608 | tf_op jit(solution)/shard_map/all_to_all | solution.py:30
  130.1 3.6 %all-to-all-start.5 = ((bf16[8,128,1,512]{1,3,2,0:T(8,128)(2,1)}), bf16[8,128,1,512]{1,3,2,0:T(8,128)(2,1)S(1)}, u32[]{:S(2)}, u32[]{:S(2)}) async-start(bf16[8,128,1,512]{1,3,2,0:T(8,128)(2,1)} %fusion.258), calls=%async_computation.5 | async-start | bytes 2097152 | tf_op jit(solution)/shard_map/all_to_all | solution.py:30
  135.5 5.6 %while.158 = (s32[]{:T(128)}, bf16[4,128,512]{1,2,0:T(8,128)(2,1)S(1)}, s32[4,512]{1,0:T(4,128)S(1)}, bf16[128,4096]{1,0:T(8,128)(2,1)S(1)}, s32[]{:T(128)}) while((s32[]{:T(128)}, bf16[4,128,512]{1,2,0:T(8,128)(2,1)S(1)}, s32[4,512]{1,0:T(4,128)S(1)}, bf16[128,4096]{1,0:T(8,128)(2,1)S(1)}, s32[]{:T(128)}) %tuple.276), condition=%wide.region_13.14_spmd.clone, body=%wide.region_12.13_spmd.clone.sunk | while | flops 541130752 | bytes 1185861 | solution.py:22
  141.2 7.6 %while.156 = (s32[]{:T(128)}, bf16[4,128,512]{1,2,0:T(8,128)(2,1)S(1)}, s32[4,512]{1,0:T(4,128)S(1)}, bf16[128,2048]{1,0:T(8,128)(2,1)}, s32[]{:T(128)}) while((s32[]{:T(128)}, bf16[4,128,512]{1,2,0:T(8,128)(2,1)S(1)}, s32[4,512]{1,0:T(4,128)S(1)}, bf16[128,2048]{1,0:T(8,128)(2,1)}, s32[]{:T(128)}) %tuple.297), condition=%wide.region_8.9_spmd.clone, body=%wide.region_7.8_spmd.clone.sunk | while | flops 270598144 | bytes 661573 | solution.py:22
  149.8 7.6 %while.159 = (s32[]{:T(128)}, bf16[4,128,512]{1,2,0:T(8,128)(2,1)S(1)}, s32[4,512]{1,0:T(4,128)S(1)}, bf16[128,2048]{1,0:T(8,128)(2,1)}, s32[]{:T(128)}) while((s32[]{:T(128)}, bf16[4,128,512]{1,2,0:T(8,128)(2,1)S(1)}, s32[4,512]{1,0:T(4,128)S(1)}, bf16[128,2048]{1,0:T(8,128)(2,1)}, s32[]{:T(128)}) %tuple.300), condition=%wide.region_15.16_spmd.clone, body=%wide.region_14.15_spmd.clone.sunk | while | flops 270598144 | bytes 661573 | solution.py:22
  160.3 5.6 %while.161 = (s32[]{:T(128)}, bf16[4,128,512]{1,2,0:T(8,128)(2,1)S(1)}, s32[4,512]{1,0:T(4,128)S(1)}, bf16[128,4096]{1,0:T(8,128)(2,1)S(1)}, s32[]{:T(128)}) while((s32[]{:T(128)}, bf16[4,128,512]{1,2,0:T(8,128)(2,1)S(1)}, s32[4,512]{1,0:T(4,128)S(1)}, bf16[128,4096]{1,0:T(8,128)(2,1)S(1)}, s32[]{:T(128)}) %tuple.285), condition=%wide.region_20.21_spmd.clone, body=%wide.region_19.20_spmd.clone.sunk | while | flops 541130752 | bytes 1185861 | solution.py:22
  166.9 7.6 %while.162 = (s32[]{:T(128)}, bf16[4,128,512]{1,2,0:T(8,128)(2,1)S(1)}, s32[4,512]{1,0:T(4,128)S(1)}, bf16[128,2048]{1,0:T(8,128)(2,1)}, s32[]{:T(128)}) while((s32[]{:T(128)}, bf16[4,128,512]{1,2,0:T(8,128)(2,1)S(1)}, s32[4,512]{1,0:T(4,128)S(1)}, bf16[128,2048]{1,0:T(8,128)(2,1)}, s32[]{:T(128)}) %tuple.303), condition=%wide.region_22.23_spmd.clone, body=%wide.region_21.22_spmd.clone.sunk | while | flops 270598144 | bytes 661573 | solution.py:22
  175.4 3.4 %while.163 = (s32[]{:T(128)}, bf16[4,128,512]{1,2,0:T(8,128)(2,1)S(1)}, s32[4,512]{1,0:T(4,128)S(1)}, bf16[128,2048]{1,0:T(8,128)(2,1)S(1)}, s32[]{:T(128)}) while((s32[]{:T(128)}, bf16[4,128,512]{1,2,0:T(8,128)(2,1)S(1)}, s32[4,512]{1,0:T(4,128)S(1)}, bf16[128,2048]{1,0:T(8,128)(2,1)S(1)}, s32[]{:T(128)}) %tuple.310), condition=%wide.region_25.26_spmd.clone, body=%wide.region_24.25_spmd.clone.sunk | while | flops 270598144 | bytes 661573 | solution.py:22
  179.6 7.5 %while.164 = (s32[]{:T(128)}, bf16[4,128,512]{1,2,0:T(8,128)(2,1)S(1)}, s32[4,512]{1,0:T(4,128)S(1)}, bf16[128,2048]{1,0:T(8,128)(2,1)}, s32[]{:T(128)}) while((s32[]{:T(128)}, bf16[4,128,512]{1,2,0:T(8,128)(2,1)S(1)}, s32[4,512]{1,0:T(4,128)S(1)}, bf16[128,2048]{1,0:T(8,128)(2,1)}, s32[]{:T(128)}) %tuple.291), condition=%wide.region_28.29_spmd.clone, body=%wide.region_27.28_spmd.clone.sunk | while | flops 270598144 | bytes 661573 | solution.py:22
  187.9 3.4 %while.165 = (s32[]{:T(128)}, bf16[4,128,512]{1,2,0:T(8,128)(2,1)S(1)}, s32[4,512]{1,0:T(4,128)S(1)}, bf16[128,2048]{1,0:T(8,128)(2,1)S(1)}, s32[]{:T(128)}) while((s32[]{:T(128)}, bf16[4,128,512]{1,2,0:T(8,128)(2,1)S(1)}, s32[4,512]{1,0:T(4,128)S(1)}, bf16[128,2048]{1,0:T(8,128)(2,1)S(1)}, s32[]{:T(128)}) %tuple.308), condition=%wide.region_31.32_spmd.clone, body=%wide.region_30.31_spmd.clone.sunk | while | flops 270598144 | bytes 661573 | solution.py:22
  196.3 7.9 %while.167 = (s32[]{:T(128)}, bf16[4,128,512]{1,2,0:T(8,128)(2,1)S(1)}, s32[4,512]{1,0:T(4,128)S(1)}, bf16[128,2048]{1,0:T(8,128)(2,1)}, s32[]{:T(128)}) while((s32[]{:T(128)}, bf16[4,128,512]{1,2,0:T(8,128)(2,1)S(1)}, s32[4,512]{1,0:T(4,128)S(1)}, bf16[128,2048]{1,0:T(8,128)(2,1)}, s32[]{:T(128)}) %tuple.311), condition=%wide.region_37.38_spmd.clone, body=%wide.region_36.37_spmd.clone.sunk | while | flops 270598144 | bytes 661573 | solution.py:22
  221.7 23.2 %reduce-scatter.2.cloned.1.call-done = f32[3,128,128]{1,2,0:T(8,128)} async-done(((f32[3,512,128]{1,2,0:T(8,128)}), f32[3,128,128]{1,2,0:T(8,128)}) %reduce-scatter.2.cloned.1.call-update) | async-done | bytes 196624 | tf_op jit(solution)/shard_map/reduce_scatter | solution.py:104
  (297 shorter events, 154.7 us)
Async XLA Ops:
  9.4 12.3 %copy-start.15 = (s32[3,2048,1]{1,2,0:T(1,128)S(1)}, s32[3,2048,1]{1,2,0:T(1,128)}, u32[]{:S(2)}) copy-start(s32[3,2048,1]{1,2,0:T(1,128)} %param.37) | copy-start | bytes 73732
  9.4 12.3 %copy-start.1 = (bf16[3,128,2048]{2,1,0:T(8,128)(2,1)S(1)}, bf16[3,128,2048]{2,1,0:T(8,128)(2,1)}, u32[]{:S(2)}) copy-start(bf16[3,128,2048]{2,1,0:T(8,128)(2,1)} %param.35) | copy-start | bytes 4718596
  14.4 20.1 %all-to-all-start = ((s32[8,1,512]{2,1,0:T(1,128)}), s32[8,1,512]{2,1,0:T(1,128)S(1)}, u32[]{:S(2)}, u32[]{:S(2)}) async-start(s32[8,1,512]{2,1,0:T(1,128)} %copy.32), calls=%async_computation | async-start | bytes 32768 | tf_op jit(solution)/shard_map/all_to_all | solution.py:73
  21.8 1.7 copy-start.16
  21.8 11.2 %copy-start.17 = (s32[8,2048]{1,0:T(8,128)S(1)}, s32[8,2048]{1,0:T(8,128)}, u32[]{:S(2)}) copy-start(s32[8,2048]{1,0:T(8,128)} %param.39) | copy-start | bytes 196612
  34.5 18.2 %all-to-all-start.2 = ((s32[8,1,512]{2,1,0:T(1,128)}), s32[8,1,512]{2,1,0:T(1,128)S(1)}, u32[]{:S(2)}, u32[]{:S(2)}) async-start(s32[8,1,512]{2,1,0:T(1,128)} %copy.35), calls=%async_computation.2 | async-start | bytes 32768 | tf_op jit(solution)/shard_map/all_to_all | solution.py:73
  52.7 16.9 %all-to-all-start.4 = ((s32[8,1,512]{2,1,0:T(1,128)}), s32[8,1,512]{2,1,0:T(1,128)S(1)}, u32[]{:S(2)}, u32[]{:S(2)}) async-start(s32[8,1,512]{2,1,0:T(1,128)} %copy.38), calls=%async_computation.4 | async-start | bytes 32768 | tf_op jit(solution)/shard_map/all_to_all | solution.py:73
  69.6 30.3 %all-to-all-start.1 = ((bf16[8,128,1,512]{1,3,2,0:T(8,128)(2,1)}), bf16[8,128,1,512]{1,3,2,0:T(8,128)(2,1)S(1)}, u32[]{:S(2)}, u32[]{:S(2)}) async-start(bf16[8,128,1,512]{1,3,2,0:T(8,128)(2,1)} %fusion.274), calls=%async_computation.1 | async-start | bytes 2097152 | tf_op jit(solution)/shard_map/all_to_all | solution.py:30
  99.9 29.2 %all-to-all-start.3 = ((bf16[8,128,1,512]{1,3,2,0:T(8,128)(2,1)}), bf16[8,128,1,512]{1,3,2,0:T(8,128)(2,1)S(1)}, u32[]{:S(2)}, u32[]{:S(2)}) async-start(bf16[8,128,1,512]{1,3,2,0:T(8,128)(2,1)} %fusion.266), calls=%async_computation.3 | async-start | bytes 2097152 | tf_op jit(solution)/shard_map/all_to_all | solution.py:30
  130.1 29.5 %all-to-all-start.5 = ((bf16[8,128,1,512]{1,3,2,0:T(8,128)(2,1)}), bf16[8,128,1,512]{1,3,2,0:T(8,128)(2,1)S(1)}, u32[]{:S(2)}, u32[]{:S(2)}) async-start(bf16[8,128,1,512]{1,3,2,0:T(8,128)(2,1)} %fusion.258), calls=%async_computation.5 | async-start | bytes 2097152 | tf_op jit(solution)/shard_map/all_to_all | solution.py:30
  133.7 111.2 %reduce-scatter.2.cloned.1.call-start = ((), (), s32[]{:S(2)}) async-start(), calls=%async_computation.7 | async-start | bytes 983040 | tf_op jit(solution)/shard_map/reduce_scatter | solution.py:104
  148.7 1.1 copy-start.2
  157.4 2.2 copy-start.4
  166.9 7.7 %copy-start.14 = (bf16[128,2048]{1,0:T(8,128)(2,1)S(1)}, bf16[128,2048]{1,0:T(8,128)(2,1)}, u32[]{:S(2)}) copy-start(bf16[128,2048]{1,0:T(8,128)(2,1)} %get-tuple-element.1258) | copy-start | bytes 1572868
  178.9 8.4 %copy-start.13 = (bf16[128,2048]{1,0:T(8,128)(2,1)S(1)}, bf16[128,2048]{1,0:T(8,128)(2,1)}, u32[]{:S(2)}) copy-start(bf16[128,2048]{1,0:T(8,128)(2,1)} %get-tuple-element.1256) | copy-start | bytes 1572868
  196.3 7.9 %copy-start.3 = (bf16[4,128,512]{1,2,0:T(8,128)(2,1)S(1)}, bf16[4,128,512]{1,2,0:T(8,128)(2,1)}, u32[]{:S(2)}) copy-start(bf16[4,128,512]{1,2,0:T(8,128)(2,1)} %copy-done.2) | copy-start | bytes 1572868
  196.3 10.1 %copy-start.5 = (bf16[4,128,512]{1,2,0:T(8,128)(2,1)S(1)}, bf16[4,128,512]{1,2,0:T(8,128)(2,1)}, u32[]{:S(2)}) copy-start(bf16[4,128,512]{1,2,0:T(8,128)(2,1)} %copy-done.4) | copy-start | bytes 1572868
  206.3 4.4 %copy-start.23 = (f32[128]{0:T(128)S(1)}, f32[128]{0:T(128)}, u32[]{:S(2)}) copy-start(f32[128]{0:T(128)} %broadcast_maximum_fusion.4) | copy-start | bytes 1540
  207.9 2.8 %copy-start.8 = (bf16[4,128,512]{1,2,0:T(8,128)(2,1)S(1)}, bf16[4,128,512]{1,2,0:T(8,128)(2,1)}, u32[]{:S(2)}) copy-start(bf16[4,128,512]{1,2,0:T(8,128)(2,1)} %copy-done.7) | copy-start | bytes 1572868
  207.9 4.3 %copy-start.22 = (f32[128]{0:T(128)S(1)}, f32[128]{0:T(128)}, u32[]{:S(2)}) copy-start(f32[128]{0:T(128)} %broadcast_maximum_fusion.3) | copy-start | bytes 1540
  209.6 4.3 %copy-start.21 = (f32[128]{0:T(128)S(1)}, f32[128]{0:T(128)}, u32[]{:S(2)}) copy-start(f32[128]{0:T(128)} %broadcast_maximum_fusion.2) | copy-start | bytes 1540
  212.2 4.5 %copy-start.12 = (bf16[4,128,512]{1,2,0:T(8,128)(2,1)S(1)}, bf16[4,128,512]{1,2,0:T(8,128)(2,1)}, u32[]{:S(2)}) copy-start(bf16[4,128,512]{1,2,0:T(8,128)(2,1)} %copy-done.11) | copy-start | bytes 1572868
  212.2 4.5 %copy-start.20 = (f32[128]{0:T(128)S(1)}, f32[128]{0:T(128)}, u32[]{:S(2)}) copy-start(f32[128]{0:T(128)} %broadcast_maximum_fusion.1) | copy-start | bytes 1540
  214.0 4.2 %copy-start.19 = (f32[128]{0:T(128)S(1)}, f32[128]{0:T(128)}, u32[]{:S(2)}) copy-start(f32[128]{0:T(128)} %broadcast_maximum_fusion) | copy-start | bytes 1540
  (7 other events, 6.0 us)
Sparse Core Ops, SparseCore 0:
  221.9 22.9 reduce-scatter.1
